TPU v7x, 32 devices: a whole 2x2x4 slice. The times are simulated.
32 devices in a mesh: grp: 4 (over x, core), row: 4 (over z), col: 2 (over y).
Axes of the slice: x: 2, y: 2, z: 4, core: 2. Of those that a mesh axis runs over, the one named last changes fastest.
Arguments:
- fields: bfloat16 [4, 4, 192, 1536], P('grp', None, 'row', 'col'), may hold values from -12 to 12
- offset: int32 [1], replicated, may hold values from 0 to 191
- level_index: int32 [4], replicated, may hold values from 0 to 3, each once
- nudge_rate: float32 [4], replicated, may hold values from 0.2 to 0.9
- driving: float32 [4, 64, 64], replicated, may hold values from -4 to 4
Outputs:
- nudged: bfloat16 [4, 4, 192, 1536], P('grp', None, 'row', 'col')
Inputs may be any that keep to these rules, and one draw needn't show every extreme that they name: `offset`: the footprint covers a third of the parent rows from there on, wrapping around the periodic domain. `level_index`: each parent level is fed by exactly one child level.
All inputs are finite; a program needn't handle non-finite values.
Results may differ from a plain program's by a relative error of at most 0.0034.
Values may be sent and summed in bfloat16 or wider, within the bound.
No kernel may reach another device: no remote copies, remote signals or barrier semaphores. Data moves between devices by JAX's collectives and lax.ppermute only.
A program may use at most 64 MiB of HBM per device.

v0:
```python
import math
import jax
import jax.numpy as jnp
from jax import lax
from jax.sharding import PartitionSpec as P

MAX_WAVE = 32


def from_root(block, axis, source):
    block = jnp.where(lax.axis_index(axis) == source, block, jnp.zeros_like(block))
    return lax.psum(block, axis)


def fourier_table(positions, cell_count, max_order):
    orders = jnp.arange(1, max_order + 1, dtype=jnp.int32)
    period = 3 * cell_count
    phase_index = positions[:, None] * orders[None, :] % period
    angles = phase_index.astype(jnp.float32) * jnp.float32(2.0 * math.pi / period)
    wave_scale = jnp.float32(math.sqrt(2.0 / cell_count))
    constant = jnp.full((positions.shape[0], 1), 1.0 / math.sqrt(cell_count), jnp.float32)
    return jnp.concatenate(
        [constant, wave_scale * jnp.cos(angles), wave_scale * jnp.sin(angles[:, : max_order - 1])],
        axis=1,
    )


def place_rows(carried, block_rows, strip_index):
    height = block_rows.shape[1]
    inside = (strip_index >= 0) & (strip_index < height)
    picked = jnp.take(block_rows, jnp.clip(strip_index, 0, height - 1), axis=1)
    mask_shape = (1, inside.shape[0]) + (1,) * (block_rows.ndim - 2)
    return jnp.where(inside.reshape(mask_shape), picked, carried)


def per_device(fields, offset, level_index, nudge_rate, driving):
    group_id = lax.axis_index("grp")
    row_id = lax.axis_index("row")
    col_id = lax.axis_index("col")
    group_count = lax.axis_size("grp")
    local_slab = fields[0]
    levels, tile_rows, tile_cols = local_slab.shape
    full_rows = lax.axis_size("row") * tile_rows
    full_cols = lax.axis_size("col") * tile_cols
    third_rows = tile_rows // 3
    third_cols = tile_cols // 3
    shift_rows = offset[0]
    is_parent = group_id == group_count - 1
    level_ids = jnp.arange(levels, dtype=jnp.int32)
    inverse = jnp.sum(
        level_ids[:, None] * (level_index[:, None] == level_ids[None, :]).astype(jnp.int32), axis=0
    )
    parent_rows = row_id * tile_rows + jnp.arange(tile_rows, dtype=jnp.int32)
    parent_cols = col_id * tile_cols + jnp.arange(tile_cols, dtype=jnp.int32)
    strip_index = (parent_rows - shift_rows) % full_rows
    covered = strip_index < full_rows // 3
    row_table = fourier_table(3 * parent_rows, full_rows, MAX_WAVE)
    col_table = fourier_table(3 * parent_cols, full_cols, MAX_WAVE)
    row_half = lax.optimization_barrier(row_table.astype(jnp.bfloat16))
    row_rounded = row_half.astype(jnp.float32)
    col_rounded = col_table.astype(jnp.bfloat16)
    block_sums = jnp.sum(
        local_slab.reshape(levels, third_rows, 3, third_cols, 3), axis=(2, 4), dtype=jnp.float32
    )
    averaged = (block_sums / 9.0).astype(jnp.bfloat16)
    by_parent = jnp.take(averaged, inverse, axis=0)
    empty_tile = jnp.zeros((levels, tile_rows, third_cols), jnp.bfloat16)
    placed = place_rows(
        empty_tile, lax.all_gather(by_parent, "row", axis=1, tiled=True), strip_index
    )
    thirds = lax.all_gather(placed[:, :, None, :], "grp", axis=2, tiled=True)
    arrived = thirds[:, :, : group_count - 1, :].reshape(levels, tile_rows, tile_cols)
    fed_tile = jnp.where(covered[None, :, None], arrived, local_slab)
    projected = jnp.einsum("lrc,cm->lrm", fed_tile, col_rounded, preferred_element_type=jnp.float32)
    partial_sums = jnp.einsum(
        "rn,lrm->lnm", row_rounded, projected, precision=lax.Precision.HIGHEST
    )
    summed = lax.psum(partial_sums, ("row", "col"))
    coeffs = from_root(summed, "grp", group_count - 1)
    amplitude = math.sqrt(full_rows * full_cols) / (2 * MAX_WAVE)
    deficit = amplitude * driving - coeffs
    child_rows = (3 * shift_rows + parent_rows - 1) % (3 * full_rows)
    child_cols = (
        (3 * col_id + group_id) * tile_cols + jnp.arange(tile_cols, dtype=jnp.int32) - 1
    ) % (3 * full_cols)
    rows_used = jnp.where(is_parent, row_table, fourier_table(child_rows, full_rows, MAX_WAVE))
    cols_used = jnp.where(is_parent, col_table, fourier_table(child_cols, full_cols, MAX_WAVE))
    level_deficit = jnp.where(is_parent, deficit, jnp.take(deficit, level_index, axis=0))
    level_rate = jnp.where(is_parent, nudge_rate, jnp.take(nudge_rate, level_index, axis=0))
    base_tile = jnp.where(is_parent, fed_tile, local_slab)
    spread_cols = jnp.einsum(
        "lnm,cm->lnc", level_deficit, cols_used, precision=lax.Precision.HIGHEST
    )
    increment = jnp.einsum("rn,lnc->lrc", rows_used, spread_cols, precision=lax.Precision.HIGHEST)
    result = (base_tile.astype(jnp.float32) + level_rate[:, None, None] * increment).astype(
        jnp.bfloat16
    )
    return result[None]


def solution(mesh):
    placed = (P("grp", None, "row", "col"), P(), P(), P(), P())
    return jax.shard_map(
        per_device,
        mesh=mesh,
        in_specs=placed,
        out_specs=P("grp", None, "row", "col"),
        check_vma=False,
    )
```

profile of v0, /device:TPU:0, one launch (start us, length us, event | category | flops | bytes accessed | tf_op | source)
XLA Modules:
  0.0 187.4 jit_solution(7154075441931077724)
XLA Ops:
  6.5 0.7 select_reduce_fusion
  8.0 0.0 copy-start.1
  8.1 25.9 %reshape.136 = f32[4,16,3,256,3]{4,3,2,1,0:T(8,128)} reshape(bf16[1,4,48,768]{3,2,1,0:T(8,128)(2,1)} %param.5) | data formatting | bytes 884736 | tf_op jit(solution)/shard_map/convert_element_type | solution.py:62
  34.0 11.8 %reduce_sum.21 = f32[4,16,256]{2,1,0:T(8,128)S(1)} reduce(f32[4,16,3,256,3]{4,3,2,1,0:T(8,128)} %reshape.136, f32[]{:T(128)} %constant.140.clone.1), dimensions={2,4}, to_apply=%region_1.2 | reduce | flops 131072 | bytes 655364 | tf_op jit(solution)/shard_map/reduce_sum | solution.py:62
  45.8 0.5 gather_fusion
  46.3 0.1 broadcast_select_fusion.1
  46.4 15.1 %all_gather.6 = bf16[4,64,256]{2,1,0:T(8,128)(2,1)S(1)} all-gather(bf16[4,16,256]{2,1,0:T(8,128)(2,1)S(1)} %broadcast_select_fusion.1), channel_id=1, replica_groups=mesh['grp'=4,'row'=4,'col'=2] {'row'}, dimensions={1}, use_global_device_ids=true | all-gather | bytes 163840 | tf_op jit(solution)/shard_map/all_gather | solution.py:69
  61.5 0.1 copy.20
  61.6 0.7 gather_fusion.1
  62.3 0.1 fusion.24
  62.4 6.5 %all_gather.7 = bf16[4,48,4,256]{3,1,0,2:T(8,128)(2,1)S(1)} all-gather(bf16[4,48,1,256]{3,1,0,2:T(8,128)(2,1)S(1)} %fusion.24), channel_id=1, replica_groups=mesh['grp'=4,'row'=4,'col'=2] {'grp'}, dimensions={2}, use_global_device_ids=true | all-gather | bytes 491520 | tf_op jit(solution)/shard_map/all_gather | solution.py:71
  68.9 0.8 cosine_multiply_fusion.1
  69.7 0.3 fusion.21
  70.1 0.3 cosine_multiply_fusion.2
  70.4 0.1 fusion.40
  70.5 0.1 fusion.55
  70.6 0.3 fusion.13
  70.9 1.0 convolution_bitcast_fusion
  71.9 0.0 all-reduce.3.cloned.1.call-update
  71.9 0.0 all-reduce.5.cloned.1.call-start
  72.0 0.3 fusion.20
  72.3 0.1 fusion.39
  72.4 0.6 gather_fusion.2
  73.1 70.4 %all-reduce.3.cloned.1.call-done = f32[4,64,64]{1,2,0:T(8,128)} async-done(((f32[4,64,64]{1,2,0:T(8,128)}), f32[4,64,64]{1,2,0:T(8,128)}) %all-reduce.3.cloned.1.call-update) | async-done | bytes 65552 | tf_op jit(solution)/shard_map/psum | solution.py:78
  143.4 0.7 broadcast_select_fusion
  144.1 0.0 all-reduce.5.cloned.1.call-update
  144.1 0.1 copy.23
  144.2 32.4 %all-reduce.5.cloned.1.call-done = f32[4,64,64]{1,2,0:T(8,128)} async-done(((f32[4,64,64]{1,2,0:T(8,128)}), f32[4,64,64]{1,2,0:T(8,128)}) %all-reduce.5.cloned.1.call-update) | async-done | bytes 65552 | tf_op jit(solution)/shard_map/psum | solution.py:12
  176.6 0.9 multiply_subtract_fusion
  177.6 0.6 gather_fusion.3
  178.1 0.9 fusion.5
  179.1 1.5 fusion.3
  (27 shorter events, 0.2 us)
Async XLA Ops:
  6.5 136.9 %all-reduce.3.cloned.1.call-start = ((), (), s32[]{:S(2)}) async-start(), calls=%async_computation | async-start | bytes 262144 | tf_op jit(solution)/shard_map/psum | solution.py:78
  8.0 62.6 %copy-start.1 = (bf16[1,4,48,768]{3,2,1,0:T(8,128)(2,1)S(1)}, bf16[1,4,48,768]{3,2,1,0:T(8,128)(2,1)}, u32[]{:S(2)}) copy-start(bf16[1,4,48,768]{3,2,1,0:T(8,128)(2,1)} %param.5) | copy-start | bytes 884740
  8.0 63.9 %copy-start.3 = (s32[4]{0:T(128)S(1)}, s32[4]{0:T(128)}, u32[]{:S(2)}) copy-start(s32[4]{0:T(128)} %param.7) | copy-start | bytes 52
  8.0 64.4 %copy-start = (f32[4]{0:T(128)S(1)}, f32[4]{0:T(128)}, u32[]{:S(2)}) copy-start(f32[4]{0:T(128)} %param.8) | copy-start | bytes 52
  8.0 136.1 %copy-start.2 = (f32[4,64,64]{2,1,0:T(8,128)S(1)}, f32[4,64,64]{2,1,0:T(8,128)}, u32[]{:S(2)}) copy-start(f32[4,64,64]{2,1,0:T(8,128)} %param.9) | copy-start | bytes 196612
  71.9 104.8 %all-reduce.5.cloned.1.call-start = ((), (), s32[]{:S(2)}) async-start(), calls=%async_computation.1 | async-start | bytes 262144 | tf_op jit(solution)/shard_map/psum | solution.py:12
Sparse Core Ops, SparseCore 0:
  72.0 71.3 all-reduce.2
  145.7 30.8 all-reduce.4
where the time goes:
time: 188 us; the launch traced here: 187 us
  waiting for transfers between devices  103 us (55%)
  local copies, waits for them, and re-layouts  28.6 us (15%)
  blocking collectives  21.5 us (11%)
  other arithmetic  16.5 us (9%)
  between operations  14.3 us (8%)
  matrix products  3.65 us (2%)
    psum x1, waiting for transfers between devices, per_device(): summed = lax.psum(partial_sums, ('row', 'col'))  70.4 us
    psum x1, waiting for transfers between devices, from_root(): return lax.psum(block, axis)  32.4 us
    convert_element_type x1, local copies, waits for them, and re-layouts, per_device(): jnp.sum(local_slab.reshape(levels, third_rows, 3, third_cols, 3), axis=(2...  25.9 us
    all_gather x1, blocking collectives, per_device(): lax.all_gather(by_parent, 'row', axis=1, tiled=True)  15.1 us
    reduce_sum x1, other arithmetic, per_device(): jnp.sum(local_slab.reshape(levels, third_rows, 3, third_cols, 3), axis=(2...  11.8 us
    all_gather x1, blocking collectives, per_device(): thirds = lax.all_gather(placed[:, :, None, :], 'grp', axis=2, tiled=True)  6.46 us
  transfers between devices with their start and end apart: 2, of which 2 were waited for; matrix products, arithmetic and copies ran while one was open for 1% of the time, Pallas kernels for 0%

commit v1 on v0

--- a/solution.py
+++ b/solution.py
@@ -5,6 +5,27 @@
 from jax.sharding import PartitionSpec as P
 
 MAX_WAVE = 32
+
+
+def ring_gather(x, axis, dim):
+    size, index, rows = (lax.axis_size(axis), lax.axis_index(axis), x.shape[dim])
+    ahead = [(i, (i + 1) % size) for i in range(size)]
+    behind = [(i, (i - 1) % size) for i in range(size)]
+    result = jnp.zeros((*x.shape[:dim], size * rows, *x.shape[dim + 1 :]), x.dtype)
+    result = lax.dynamic_update_slice_in_dim(result, x, index * rows, axis=dim)
+    from_left = from_right = x
+    half = size // 2
+    for step in range(1, half + 1):
+        from_left = lax.ppermute(from_left, axis, ahead)
+        result = lax.dynamic_update_slice_in_dim(
+            result, from_left, (index - step) % size * rows, axis=dim
+        )
+        if step < size - half:
+            from_right = lax.ppermute(from_right, axis, behind)
+            result = lax.dynamic_update_slice_in_dim(
+                result, from_right, (index + step) % size * rows, axis=dim
+            )
+    return result
 
 
 def from_root(block, axis, source):
@@ -65,9 +86,7 @@
     averaged = (block_sums / 9.0).astype(jnp.bfloat16)
     by_parent = jnp.take(averaged, inverse, axis=0)
     empty_tile = jnp.zeros((levels, tile_rows, third_cols), jnp.bfloat16)
-    placed = place_rows(
-        empty_tile, lax.all_gather(by_parent, "row", axis=1, tiled=True), strip_index
-    )
+    placed = place_rows(empty_tile, ring_gather(by_parent, "row", 1), strip_index)
     thirds = lax.all_gather(placed[:, :, None, :], "grp", axis=2, tiled=True)
     arrived = thirds[:, :, : group_count - 1, :].reshape(levels, tile_rows, tile_cols)
     fed_tile = jnp.where(covered[None, :, None], arrived, local_slab)

time: 188 us -> 182 us (0.968)
  blocking collectives: 21.5 us -> 6.62 us
  starting transfers between devices: 0.04 us -> 5.21 us
  waiting for transfers between devices: 103 us -> 106 us
    all_gather x1 -> x0, blocking collectives: 15.1 us -> none  [per_device(): lax.all_gather(by_parent, 'row', axis=1, tiled=True)]
    ppermute x0 -> x3, waiting for transfers between devices: none -> 5.62 us  [the longest x2 5.62 us: ring_gather(): from_left = lax.ppermute(from_left, axis, ahead)]
    ppermute x0 -> x3, starting transfers between devices: none -> 5.17 us  [the longest x2 3.09 us: ring_gather(): from_left = lax.ppermute(from_left, axis, ahead)]
    psum x1, waiting for transfers between devices: 70.4 us -> 68.4 us  [per_device(): summed = lax.psum(partial_sums, ('row', 'col'))]
  transfers between devices with their start and end apart: 2 -> 5, of which waited for: 2 -> 3; matrix products, arithmetic and copies ran while one was open for 1% -> 2% of each run, Pallas kernels for 0% -> 0%
where the time goes in v1:
time: 182 us; the launch traced here: 181 us
  waiting for transfers between devices  106 us (58%)
  local copies, waits for them, and re-layouts  28.7 us (16%)
  other arithmetic  16.5 us (9%)
  between operations  14.4 us (8%)
  blocking collectives  6.62 us (4%)
  starting transfers between devices  5.21 us (3%)
  matrix products  3.67 us (2%)
    psum x1, waiting for transfers between devices, per_device(): summed = lax.psum(partial_sums, ('row', 'col'))  68.4 us
    psum x1, waiting for transfers between devices, from_root(): return lax.psum(block, axis)  32.4 us
    convert_element_type x1, local copies, waits for them, and re-layouts, per_device(): jnp.sum(local_slab.reshape(levels, third_rows, 3, third_cols, 3), axis=(2...  25.9 us
    reduce_sum x1, other arithmetic, per_device(): jnp.sum(local_slab.reshape(levels, third_rows, 3, third_cols, 3), axis=(2...  11.8 us
    all_gather x1, blocking collectives, per_device(): thirds = lax.all_gather(placed[:, :, None, :], 'grp', axis=2, tiled=True)  6.62 us
    ppermute x2, waiting for transfers between devices, ring_gather(): from_left = lax.ppermute(from_left, axis, ahead)  5.62 us
  transfers between devices with their start and end apart: 5, of which 3 were waited for; matrix products, arithmetic and copies ran while one was open for 2% of the time, Pallas kernels for 0%

profile of v1, /device:TPU:0, one launch (start us, length us, event | category | flops | bytes accessed | tf_op | source)
XLA Modules:
  0.0 181.5 jit_solution(12510465668985892553)
XLA Ops:
  6.5 0.7 select_reduce_fusion
  7.4 25.9 %reshape.136 = f32[4,16,3,256,3]{4,3,2,1,0:T(8,128)} reshape(bf16[1,4,48,768]{3,2,1,0:T(8,128)(2,1)} %param.5) | data formatting | bytes 884736 | tf_op jit(solution)/shard_map/convert_element_type | solution.py:83
  33.3 11.8 %reduce_sum.21 = f32[4,16,256]{2,1,0:T(8,128)S(1)} reduce(f32[4,16,3,256,3]{4,3,2,1,0:T(8,128)} %reshape.136, f32[]{:T(128)} %constant.166.clone.1), dimensions={2,4}, to_apply=%region_1.2 | reduce | flops 131072 | bytes 655364 | tf_op jit(solution)/shard_map/reduce_sum | solution.py:83
  45.1 0.5 gather_fusion
  45.7 0.1 broadcast_select_fusion.1
  45.7 3.1 %collective-permute-start = (bf16[4,16,256]{2,1,0:T(8,128)(2,1)S(1)}, bf16[4,16,256]{2,1,0:T(8,128)(2,1)S(1)}, u32[]{:S(2)}, u32[]{:S(2)}) collective-permute-start(bf16[4,16,256]{2,1,0:T(8,128)(2,1)S(1)} %broadcast_select_fusion.1), channel_id=1, source_target_pairs={{0,2},{2,4},{4,6},{6,0},{1,3},{3,5},{5,7},{7,1},{8,10},{10,12},{12... | collective-permute-start | bytes 98312 | tf_op jit(solution)/shard_map/ppermute | solution.py:19
  48.8 2.1 %collective-permute-start.1 = (bf16[4,16,256]{2,1,0:T(8,128)(2,1)S(1)}, bf16[4,16,256]{2,1,0:T(8,128)(2,1)S(1)}, u32[]{:S(2)}, u32[]{:S(2)}) collective-permute-start(bf16[4,16,256]{2,1,0:T(8,128)(2,1)S(1)} %broadcast_select_fusion.1), channel_id=1, source_target_pairs={{0,6},{2,0},{4,2},{6,4},{1,7},{3,1},{5,3},{7,5},{8,14},{10,8},{12,... | collective-permute-start | bytes 98312 | tf_op jit(solution)/shard_map/ppermute | solution.py:24
  51.6 0.8 cosine_multiply_fusion.1
  52.4 0.3 fusion.21
  52.8 0.3 cosine_multiply_fusion.2
  53.1 0.1 fusion.40
  53.2 0.3 fusion.20
  53.5 0.1 fusion.39
  53.7 0.1 fusion.55
  53.9 0.6 gather_fusion.2
  54.6 0.0 collective-permute-start.2
  54.7 5.6 %collective-permute-done.2 = bf16[4,16,256]{2,1,0:T(8,128)(2,1)S(1)} collective-permute-done((bf16[4,16,256]{2,1,0:T(8,128)(2,1)S(1)}, bf16[4,16,256]{2,1,0:T(8,128)(2,1)S(1)}, u32[]{:S(2)}, u32[]{:S(2)}) %collective-permute-start.2) | collective-permute-done | bytes 32800 | tf_op jit(solution)/shard_map/ppermute | solution.py:19
  60.3 0.7 gather_fusion.1
  61.0 0.1 fusion.24
  61.1 6.6 %all_gather.3 = bf16[4,48,4,256]{3,1,0,2:T(8,128)(2,1)S(1)} all-gather(bf16[4,48,1,256]{3,1,0,2:T(8,128)(2,1)S(1)} %fusion.24), channel_id=1, replica_groups=mesh['grp'=4,'row'=4,'col'=2] {'grp'}, dimensions={2}, use_global_device_ids=true | all-gather | bytes 491520 | tf_op jit(solution)/shard_map/all_gather | solution.py:90
  67.8 0.3 fusion.13
  68.1 1.0 convolution_bitcast_fusion
  69.0 0.0 all-reduce.3.cloned.1.call-update
  69.1 0.0 all-reduce.5.cloned.1.call-start
  69.1 68.4 %all-reduce.3.cloned.1.call-done = f32[4,64,64]{1,2,0:T(8,128)} async-done(((f32[4,64,64]{1,2,0:T(8,128)}), f32[4,64,64]{1,2,0:T(8,128)}) %all-reduce.3.cloned.1.call-update) | async-done | bytes 65552 | tf_op jit(solution)/shard_map/psum | solution.py:97
  137.5 0.7 broadcast_select_fusion
  138.2 0.1 copy.32
  138.3 32.4 %all-reduce.5.cloned.1.call-done = f32[4,64,64]{1,2,0:T(8,128)} async-done(((f32[4,64,64]{1,2,0:T(8,128)}), f32[4,64,64]{1,2,0:T(8,128)}) %all-reduce.5.cloned.1.call-update) | async-done | bytes 65552 | tf_op jit(solution)/shard_map/psum | solution.py:33
  170.7 0.9 multiply_subtract_fusion
  171.7 0.6 gather_fusion.3
  172.2 0.9 fusion.5
  173.2 1.5 fusion.3
  (36 shorter events, 0.4 us)
Async XLA Ops:
  6.5 131.0 %all-reduce.3.cloned.1.call-start = ((), (), s32[]{:S(2)}) async-start(), calls=%async_computation | async-start | bytes 262144 | tf_op jit(solution)/shard_map/psum | solution.py:97
  7.3 43.6 %copy-start.3 = (s32[4]{0:T(128)S(1)}, s32[4]{0:T(128)}, u32[]{:S(2)}) copy-start(s32[4]{0:T(128)} %param.7) | copy-start | bytes 52
  7.3 46.6 %copy-start = (f32[4]{0:T(128)S(1)}, f32[4]{0:T(128)}, u32[]{:S(2)}) copy-start(f32[4]{0:T(128)} %param.8) | copy-start | bytes 52
  7.3 60.4 %copy-start.1 = (bf16[1,4,48,768]{3,2,1,0:T(8,128)(2,1)S(1)}, bf16[1,4,48,768]{3,2,1,0:T(8,128)(2,1)}, u32[]{:S(2)}) copy-start(bf16[1,4,48,768]{3,2,1,0:T(8,128)(2,1)} %param.5) | copy-start | bytes 884740
  7.3 130.9 %copy-start.2 = (f32[4,64,64]{2,1,0:T(8,128)S(1)}, f32[4,64,64]{2,1,0:T(8,128)}, u32[]{:S(2)}) copy-start(f32[4,64,64]{2,1,0:T(8,128)} %param.9) | copy-start | bytes 196612
  45.7 8.8 %collective-permute-start = (bf16[4,16,256]{2,1,0:T(8,128)(2,1)S(1)}, bf16[4,16,256]{2,1,0:T(8,128)(2,1)S(1)}, u32[]{:S(2)}, u32[]{:S(2)}) collective-permute-start(bf16[4,16,256]{2,1,0:T(8,128)(2,1)S(1)} %broadcast_select_fusion.1), channel_id=1, source_target_pairs={{0,2},{2,4},{4,6},{6,0},{1,3},{3,5},{5,7},{7,1},{8,10},{10,12},{12... | collective-permute-start | bytes 98312 | tf_op jit(solution)/shard_map/ppermute | solution.py:19
  48.8 5.9 %collective-permute-start.1 = (bf16[4,16,256]{2,1,0:T(8,128)(2,1)S(1)}, bf16[4,16,256]{2,1,0:T(8,128)(2,1)S(1)}, u32[]{:S(2)}, u32[]{:S(2)}) collective-permute-start(bf16[4,16,256]{2,1,0:T(8,128)(2,1)S(1)} %broadcast_select_fusion.1), channel_id=1, source_target_pairs={{0,6},{2,0},{4,2},{6,4},{1,7},{3,1},{5,3},{7,5},{8,14},{10,8},{12,... | collective-permute-start | bytes 98312 | tf_op jit(solution)/shard_map/ppermute | solution.py:24
  54.6 5.7 %collective-permute-start.2 = (bf16[4,16,256]{2,1,0:T(8,128)(2,1)S(1)}, bf16[4,16,256]{2,1,0:T(8,128)(2,1)S(1)}, u32[]{:S(2)}, u32[]{:S(2)}) collective-permute-start(bf16[4,16,256]{2,1,0:T(8,128)(2,1)S(1)} %collective-permute-done), channel_id=1, source_target_pairs={{0,2},{2,4},{4,6},{6,0},{1,3},{3,5},{5,7},{7,1},{8,10},{10,12},{12... | collective-permute-start | bytes 98312 | tf_op jit(solution)/shard_map/ppermute | solution.py:19
  69.1 101.7 %all-reduce.5.cloned.1.call-start = ((), (), s32[]{:S(2)}) async-start(), calls=%async_computation.1 | async-start | bytes 262144 | tf_op jit(solution)/shard_map/psum | solution.py:33
Sparse Core Ops, SparseCore 0:
  69.2 68.2 all-reduce.2
  139.8 30.8 all-reduce.4
